TPU v7x, 32 devices: a whole 2x2x4 slice. The times are simulated.
32 devices in a mesh: ta: 16 (over z, x, core), aa: 2 (over y).
Axes of the slice: x: 2, y: 2, z: 4, core: 2. Of those that a mesh axis runs over, the one named last changes fastest.
Arguments:
- voltages: bfloat16 [256, 393216], P('aa', 'ta'), may hold values from -6 to 6
- pfb_window: float32 [4, 8192], replicated, may hold values from -3 to 3
Outputs:
- visibilities: float32 [2048, 256, 512], P('ta', 'aa')
All inputs are finite; a program needn't handle non-finite values.
Results may differ from a plain program's by a relative error of at most 0.0026.
Values may be sent and summed in bfloat16 or wider, within the bound.
A program may use at most 192 MiB of HBM per device.

v0:
```python
import math
import jax
import jax.numpy as jnp
from jax import lax
from jax.sharding import PartitionSpec as P

NFFT = 8192
CH = 2048
TAPS = 4
CH_OFF = 1024


def shifted(x, axis, by):
    peers = lax.axis_size(axis)
    pairs = [(i, i + by) for i in range(peers) if 0 <= i + by < peers]
    return lax.ppermute(x, axis, pairs)


def tables(row_count, col_count, modulus, offset):
    row_index = lax.broadcasted_iota(jnp.int32, (row_count, col_count), 0)
    col_index = lax.broadcasted_iota(jnp.int32, (row_count, col_count), 1) + offset
    phases = row_index * col_index % modulus
    angles = phases.astype(jnp.float32) * (2.0 * math.pi / modulus)
    return (jnp.cos(angles), jnp.sin(angles))


def with_quadrature(spectra):
    swapped = jnp.stack([spectra[:, :, 1], -spectra[:, :, 0]], axis=2)
    return jnp.concatenate([spectra, swapped], axis=3)


def products(left_rows, right_cols):
    return jnp.einsum("cfpi,cfpj->cij", left_rows, right_cols, preferred_element_type=jnp.float32)


def channelize(filtered):
    signal_count = filtered.shape[0]
    frame_count = filtered.shape[1]
    section_one = 64
    section_two = NFFT // section_one
    highest = lax.Precision.HIGHEST
    blocks = filtered.reshape(signal_count, frame_count, section_one, section_two)
    cosine_one, sine_one = tables(section_one, section_one, section_one, 0)
    section_real = jnp.einsum("sfan,ak->sfkn", blocks, cosine_one, precision=highest)
    section_imag = -jnp.einsum("sfan,ak->sfkn", blocks, sine_one, precision=highest)
    cosine_twist, sine_twist = tables(section_one, section_two, NFFT, 0)
    twist_real = section_real * cosine_twist + section_imag * sine_twist
    twist_imag = section_imag * cosine_twist - section_real * sine_twist
    cosine_two, sine_two = tables(
        section_two, CH // section_one, section_two, CH_OFF // section_one
    )
    scaling = 1.0 / math.sqrt(NFFT)
    spec_real = (
        jnp.einsum("sfkn,nm->mkfs", twist_real, cosine_two, precision=highest)
        + jnp.einsum("sfkn,nm->mkfs", twist_imag, sine_two, precision=highest)
    ) * scaling
    spec_imag = (
        jnp.einsum("sfkn,nm->mkfs", twist_imag, cosine_two, precision=highest)
        - jnp.einsum("sfkn,nm->mkfs", twist_real, sine_two, precision=highest)
    ) * scaling
    return jnp.stack([spec_real, spec_imag], axis=3).reshape(CH, frame_count, 2, signal_count)


def filter_frames(extended, pfb_window, frame_count):
    filtered = jnp.zeros((extended.shape[0], frame_count, NFFT), jnp.float32)
    for tap_index in range(TAPS):
        filtered = filtered + pfb_window[tap_index] * extended[
            :, tap_index : tap_index + frame_count, :
        ].astype(jnp.float32)
    return filtered


def per_device(voltages, pfb_window):
    signal_count = voltages.shape[0]
    frame_count = voltages.shape[1] // NFFT
    history = shifted(voltages, "ta", 1)
    extended = jnp.concatenate([history, voltages], axis=1).reshape(
        signal_count, frame_count + TAPS - 1, NFFT
    )
    filtered = filter_frames(extended, pfb_window, frame_count)
    spectra = channelize(filtered).astype(jnp.bfloat16)
    owned = lax.all_to_all(spectra, "ta", split_axis=0, concat_axis=1, tiled=True)
    frames_all = owned.shape[1]
    norm_scale = 1.0 / math.sqrt(frames_all)
    left_rows = with_quadrature(owned)
    result = products(left_rows, lax.all_gather(owned, "aa", axis=3, tiled=True)) * norm_scale
    return jnp.concatenate([result[:, :signal_count], result[:, signal_count:]], axis=2)


def solution(mesh):
    in_specs = (P("aa", "ta"), P())
    out_specs = P("ta", "aa", None)
    return jax.shard_map(
        per_device, mesh=mesh, in_specs=in_specs, out_specs=out_specs, check_vma=False
    )
```

profile of v0, /device:TPU:0, one launch (start us, length us, event | category | flops | bytes accessed | tf_op | source)
XLA Modules:
  0.0 537.9 jit_solution(2451833652315403954)
XLA Ops:
  6.5 8.6 %copy.43 = bf16[128,24576]{0,1:T(8,128)(2,1)} copy(bf16[128,24576]{1,0:T(8,128)(2,1)} %param.2) | data formatting | bytes 12582912 | tf_op args[0]
  15.2 2.8 collective-permute-start
  18.0 0.1 fusion.48
  18.1 0.1 fusion.88
  18.2 9.3 %collective-permute-done = bf16[128,24576]{0,1:T(8,128)(2,1)S(1)} collective-permute-done((bf16[128,24576]{0,1:T(8,128)(2,1)}, bf16[128,24576]{0,1:T(8,128)(2,1)S(1)}, u32[]{:S(2)}, u32[]{:S(2)}) %collective-permute-start) | collective-permute-done | bytes 6291488 | tf_op jit(solution)/shard_map/ppermute | solution.py:16
  27.5 24.4 %pad_maximum_fusion.1 = bf16[128,49152]{0,1:T(8,128)(2,1)S(1)} fusion(bf16[128,24576]{0,1:T(8,128)(2,1)} %copy.43, bf16[128,24576]{0,1:T(8,128)(2,1)S(1)} %collective-permute-done), kind=kLoop, calls=%fused_computation.2 | loop fusion | flops 25165824 | bytes 25165824 | tf_op jit(solution)/shard_map/concatenate | solution.py:77
  52.0 8.4 %multiply_add_fusion = f32[128,3,8192]{0,2,1:T(8,128)} fusion(bf16[128,6,8192]{0,2,1:T(8,128)(2,1)S(1)} %bitcast.52, f32[8192]{0:T(1024)S(1)} %bitcast.62, f32[8192]{0:T(1024)S(1)} %bitcast.63, f32[8192]{0:T(1024)S(1)} %bitcast.61, f32[8192]{0:T(1024)S(1)} %bitcast.60), kind=kLoop, calls=%fused_computation.5 | loop fusion | flops 34603008 | bytes 37879808 | tf_op jit(solution)/shard_map/add | solution.py:67
  60.4 12.8 %copy.45 = f32[128,3,64,128]{3,2,1,0:T(8,128)} copy(f32[128,3,64,128]{0,3,2,1:T(8,128)} %bitcast.55) | data formatting | bytes 25165824 | tf_op jit(solution)/shard_map/reshape | solution.py:42
  73.2 16.9 %fusion.29 = f32[64,128,3,128]{3,0,2,1:T(8,128)} fusion(f32[128,3,64,128]{3,2,1,0:T(8,128)} %copy.45), kind=kOutput, calls=%fused_computation.37 | convolution fusion | flops 2415976448 | bytes 25165824 | tf_op jit(solution)/shard_map/sfan,ak->sfkn/dot_general | solution.py:45
  90.1 23.8 %add_bitcast_fusion = (f32[128,3,64,128]{3,2,1,0:T(8,128)}, f32[128,3,64,128]{3,2,1,0:T(8,128)}) fusion(f32[64,128,3,128]{3,0,2,1:T(8,128)} %fusion.29, f32[64,128]{1,0:T(8,128)S(1)} %get-tuple-element.15, f32[64,128]{1,0:T(8,128)S(1)} %get-tuple-element.16, f32[128,3,64,128]{3,2,1,0:T(8,128)} %copy.45), kind=kOutput, calls=%fused_computation.4 | convolution fusion | flops 2437996544 | bytes 50397184 | tf_op jit(solution)/shard_map/sfan,ak->sfkn/dot_general | solution.py:44
  113.9 22.7 %fusion = f32[32,128,3,64]{1,0,3,2:T(8,128)S(1)} fusion(f32[128,3,64,128]{3,2,1,0:T(8,128)} %get-tuple-element.8, s32[32]{0:T(128)S(1)} %iota_add_fusion), kind=kOutput, calls=%fused_computation.6 | convolution fusion | flops 1208016896 | bytes 15728768 | tf_op jit(solution)/shard_map/sfkn,nm->mkfs/dot_general | solution.py:58
  136.6 0.0 copy-done
  136.6 0.0 slice-start.2
  136.6 18.4 %fusion.2 = f32[32,128,3,64]{1,0,3,2:T(8,128)S(1)} fusion(f32[128,3,64,128]{3,2,1,0:T(8,128)S(1)} %copy-done, s32[32]{0:T(128)S(1)} %iota_add_fusion), kind=kOutput, calls=%fused_computation.8 | convolution fusion | flops 1208016896 | bytes 15728768 | tf_op jit(solution)/shard_map/sfkn,nm->mkfs/dot_general | solution.py:55
  155.1 0.0 slice-done
  155.1 18.3 %fusion.17 = bf16[32,64,3,128]{3,0,1,2:T(8,128)(2,1)S(1)} fusion(f32[32,128,3,64]{1,0,3,2:T(8,128)S(1)} %fusion.2, f32[128,3,64,128]{3,2,1,0:T(8,128)S(1)} %bitcast.54, s32[32]{0:T(128)S(1)} %iota_add_fusion), kind=kOutput, calls=%fused_computation.23 | convolution fusion | flops 1210376192 | bytes 17301632 | tf_op jit(solution)/shard_map/sfkn,nm->mkfs/dot_general | solution.py:54
  173.5 18.7 %fusion.20 = bf16[32,64,3,128]{3,0,1,2:T(8,128)(2,1)S(1)} fusion(f32[32,128,3,64]{1,0,3,2:T(8,128)S(1)} %fusion, f32[128,3,64,128]{3,2,1,0:T(8,128)S(1)} %bitcast.54, s32[32]{0:T(128)S(1)} %iota_add_fusion), kind=kOutput, calls=%fused_computation.24 | convolution fusion | flops 1210376192 | bytes 17301632 | tf_op jit(solution)/shard_map/sfkn,nm->mkfs/dot_general | solution.py:59
  192.2 0.6 copy.52
  192.8 0.6 copy.49
  193.4 0.3 pad_maximum_fusion.2
  193.7 28.6 %copy.53 = bf16[2048,3,2,128]{3,2,1,0:T(2,128)(2,1)S(1)} copy(bf16[2048,3,2,128]{3,0,1,2:T(8,128)(2,1)S(1)} %pad_maximum_fusion.2) | data formatting | bytes 6291456 | tf_op jit(solution)/shard_map/stack | solution.py:61
  222.3 136.9 %all_to_all.18 = bf16[2048,3,2,128]{3,2,1,0:T(2,128)(2,1)S(1)} all-to-all(bf16[2048,3,2,128]{3,2,1,0:T(2,128)(2,1)S(1)} %copy.53), channel_id=1, replica_groups=mesh['ta'=16,'aa'=2] {'ta'}, dimensions={0} | all-to-all | bytes 6291456 | tf_op jit(solution)/shard_map/all_to_all | solution.py:82
  359.2 0.4 copy.54
  359.6 0.4 copy.55
  360.0 3.7 copy.58
  363.8 0.0 all-gather.2.cloned.1.call-update
  363.8 2.2 fusion.87
  366.0 78.9 %all-gather.2.cloned.1.call-done = bf16[128,48,2,256]{3,1,2,0:T(8,128)(2,1)} async-done(((bf16[128,48,2,128]{3,1,2,0:T(8,128)(2,1)}), bf16[128,48,2,256]{3,1,2,0:T(8,128)(2,1)}) %all-gather.2.cloned.1.call-update) | async-done | bytes 6291472 | tf_op jit(solution)/shard_map/all_gather | solution.py:86
  444.9 16.4 %bitcast_multiply_fusion = f32[128,256,256]{1,2,0:T(8,128)} fusion(bf16[128,48,2,256]{3,1,2,0:T(8,128)(2,1)} %all-gather.2.cloned.1.call-done, bf16[128,48,1,128]{3,1,2,0:T(8,128)(2,1)S(1)} %get-tuple-element.10, bf16[128,48,1,128]{3,1,2,0:T(8,128)(2,1)S(1)} %get-tuple-element.9, bf16[128,48,2,128]{3,1,2,0:T(8,128)(2,1)} %copy.58), kind=kOutput, calls=%fused_computation.1 | convolution fusion | flops 1637875712 | bytes 46137344 | tf_op jit(solution)/shard_map/cfpi,cfpj->cij/dot_general | solution.py:33
  461.3 17.7 %fusion.86 = (f32[128,128,256]{1,2,0:T(8,128)S(1)}, f32[128,128,256]{1,2,0:T(8,128)}) fusion(f32[128,256,256]{1,2,0:T(8,128)} %bitcast_multiply_fusion), kind=kLoop, calls=%fused_computation.92 | loop fusion | bytes 67108864 | tf_op jit(solution)/shard_map/slice | solution.py:87
  479.0 18.3 %pad_maximum_fusion = f32[128,128,512]{1,2,0:T(8,128)} fusion(f32[128,128,256]{1,2,0:T(8,128)} %get-tuple-element.6, f32[128,128,256]{1,2,0:T(8,128)S(1)} %get-tuple-element.5), kind=kLoop, calls=%fused_computation | loop fusion | flops 8388608 | bytes 67108864 | tf_op jit(solution)/shard_map/concatenate | solution.py:87
  497.4 33.4 %copy.60 = f32[128,128,512]{2,1,0:T(8,128)} copy(f32[128,128,512]{1,2,0:T(8,128)} %pad_maximum_fusion) | data formatting | bytes 67108864 | tf_op jit(solution)/shard_map/concatenate | solution.py:87
  (10 shorter events, 0.0 us)
Async XLA Ops:
  6.5 11.6 %copy-start.1 = (f32[4,8192]{1,0:T(4,128)S(1)}, f32[4,8192]{1,0:T(4,128)}, u32[]{:S(2)}) copy-start(f32[4,8192]{1,0:T(4,128)} %param.3) | copy-start | bytes 393220
  6.5 438.3 %all-gather.2.cloned.1.call-start = ((), (), s32[]{:S(2)}) async-start(), calls=%async_computation.1 | async-start | bytes 9437184 | tf_op jit(solution)/shard_map/all_gather | solution.py:86
  15.2 12.4 %collective-permute-start = (bf16[128,24576]{0,1:T(8,128)(2,1)}, bf16[128,24576]{0,1:T(8,128)(2,1)S(1)}, u32[]{:S(2)}, u32[]{:S(2)}) collective-permute-start(bf16[128,24576]{0,1:T(8,128)(2,1)} %copy.43), channel_id=1, source_target_pairs={{0,2},{2,4},{4,6},{6,8},{8,10},{10,12},{12,14},{14,16},{16,18},{18... | collective-permute-start | bytes 18874376 | tf_op jit(solution)/shard_map/ppermute | solution.py:16
  113.8 22.8 %copy-start = (f32[128,3,64,128]{3,2,1,0:T(8,128)S(1)}, f32[128,3,64,128]{3,2,1,0:T(8,128)}, u32[]{:S(2)}) copy-start(f32[128,3,64,128]{3,2,1,0:T(8,128)} %get-tuple-element.8) | copy-start | bytes 37748740
  113.9 41.2 %slice-start = ((s8[12582912]{0:T(1024)(128)(4,1)}), s8[4194304]{0:T(1024)(128)(4,1)S(1)}, s32[]{:S(2)}) async-start(s8[12582912]{0:T(1024)(128)(4,1)} %bitcast.53), calls=%async_computation.2 | async-start | bytes 8388608
  113.9 41.2 %slice-start.1 = ((s8[12582912]{0:T(1024)(128)(4,1)}), s8[4194304]{0:T(1024)(128)(4,1)S(1)}, s32[]{:S(2)}) async-start(s8[12582912]{0:T(1024)(128)(4,1)} %bitcast.53), calls=%async_computation.3 | async-start | bytes 8388608
  136.6 18.5 %slice-start.2 = ((s8[12582912]{0:T(1024)(128)(4,1)}), s8[4194304]{0:T(1024)(128)(4,1)S(1)}, s32[]{:S(2)}) async-start(s8[12582912]{0:T(1024)(128)(4,1)} %bitcast.53), calls=%async_computation.4 | async-start | bytes 8388608
Sparse Core Ops, SparseCore 0:
  363.9 80.9 all-gather.1
where the time goes:
time: 548 us; the launch traced here: 538 us
  blocking collectives  137 us (25%)
  matrix products  135 us (25%)
  local copies, waits for them, and re-layouts  107 us (20%)
  waiting for transfers between devices  88.2 us (16%)
  other arithmetic  53.9 us (10%)
  between operations  13.8 us (3%)
    all_to_all x1, blocking collectives, per_device(): lax.all_to_all(spectra, 'ta', split_axis=0, concat_axis=1, tiled=True)  137 us
    all_gather x1, waiting for transfers between devices, per_device(): lax.all_gather(owned, 'aa', axis=3, tiled=True)  78.9 us
    concatenate x1, local copies, waits for them, and re-layouts, per_device(): jnp.concatenate([result[:, :signal_count], result[:, signal_count:]], axi...  33.4 us
    another operation x1, local copies, waits for them, and re-layouts, channelize(): jnp.stack([spec_real, spec_imag], axis=3)  28.6 us
    concatenate x1, other arithmetic, per_device(): jnp.concatenate([history, voltages], axis=1)  24.4 us
    dot_general x1, matrix products, channelize(): jnp.einsum('sfan,ak->sfkn', blocks, cosine_one, precision=highest)  23.8 us
    dot_general x1, matrix products, channelize(): jnp.einsum('sfkn,nm->mkfs', twist_imag, cosine_two, precision=highest)  22.7 us
    dot_general x1, matrix products, channelize(): jnp.einsum('sfkn,nm->mkfs', twist_real, sine_two, precision=highest)  18.7 us
  transfers between devices with their start and end apart: 2, of which 2 were waited for; matrix products, arithmetic and copies ran while one was open for 0% of the time, Pallas kernels for 0%

commit v1 on v0

--- a/solution.py
+++ b/solution.py
@@ -79,7 +79,10 @@
     )
     filtered = filter_frames(extended, pfb_window, frame_count)
     spectra = channelize(filtered).astype(jnp.bfloat16)
-    owned = lax.all_to_all(spectra, "ta", split_axis=0, concat_axis=1, tiled=True)
+    owned = jnp.concatenate(
+        lax.all_to_all(jnp.stack(jnp.split(spectra, lax.axis_size("ta"), axis=0)), "ta", 0, 0),
+        axis=1,
+    )
     frames_all = owned.shape[1]
     norm_scale = 1.0 / math.sqrt(frames_all)
     left_rows = with_quadrature(owned)

time: 548 us -> 523 us (0.954)
  local copies, waits for them, and re-layouts: 107 us -> 79.9 us
    another operation x1 -> x0, local copies, waits for them, and re-layouts: 28.6 us -> none  [channelize(): jnp.stack([spec_real, spec_imag], axis=3)]
where the time goes in v1:
time: 523 us; the launch traced here: 514 us
  matrix products  139 us (27%)
  blocking collectives  137 us (26%)
  waiting for transfers between devices  86.5 us (17%)
  local copies, waits for them, and re-layouts  79.9 us (15%)
  other arithmetic  53.8 us (10%)
  between operations  14.1 us (3%)
    all_to_all x1, blocking collectives, per_device(): lax.all_to_all(jnp.stack(jnp.split(spectra, lax.axis_size('ta'), axis=0))...  137 us
    all_gather x1, waiting for transfers between devices, per_device(): lax.all_gather(owned, 'aa', axis=3, tiled=True)  77.2 us
    concatenate x1, local copies, waits for them, and re-layouts, per_device(): jnp.concatenate([result[:, :signal_count], result[:, signal_count:]], axi...  33.4 us
    concatenate x1, other arithmetic, per_device(): jnp.concatenate([history, voltages], axis=1)  24.4 us
    dot_general x1, matrix products, channelize(): jnp.einsum('sfan,ak->sfkn', blocks, cosine_one, precision=highest)  24 us
    dot_general x1, matrix products, channelize(): jnp.einsum('sfkn,nm->mkfs', twist_imag, sine_two, precision=highest)  22.9 us
    dot_general x1, matrix products, channelize(): jnp.einsum('sfkn,nm->mkfs', twist_imag, cosine_two, precision=highest)  22.5 us
    dot_general x1, matrix products, channelize(): jnp.einsum('sfkn,nm->mkfs', twist_real, sine_two, precision=highest)  18.4 us
  transfers between devices with their start and end apart: 2, of which 2 were waited for; matrix products, arithmetic and copies ran while one was open for 0% of the time, Pallas kernels for 0%

profile of v1, /device:TPU:0, one launch (start us, length us, event | category | flops | bytes accessed | tf_op | source)
XLA Modules:
  0.0 513.6 jit_solution(2793445585837645934)
XLA Ops:
  6.5 0.0 all-gather.2.cloned.1.call-start
  6.5 8.6 %copy.23 = bf16[128,24576]{0,1:T(8,128)(2,1)} copy(bf16[128,24576]{1,0:T(8,128)(2,1)} %param.2) | data formatting | bytes 12582912 | tf_op args[0]
  15.2 2.8 collective-permute-start
  18.0 0.1 fusion.65
  18.1 0.0 copy-done.1
  18.1 0.1 fusion.105
  18.2 9.3 %collective-permute-done = bf16[128,24576]{0,1:T(8,128)(2,1)S(1)} collective-permute-done((bf16[128,24576]{0,1:T(8,128)(2,1)}, bf16[128,24576]{0,1:T(8,128)(2,1)S(1)}, u32[]{:S(2)}, u32[]{:S(2)}) %collective-permute-start) | collective-permute-done | bytes 6291488 | tf_op jit(solution)/shard_map/ppermute | solution.py:16
  27.5 24.4 %pad_maximum_fusion.1 = bf16[128,49152]{0,1:T(8,128)(2,1)S(1)} fusion(bf16[128,24576]{0,1:T(8,128)(2,1)} %copy.23, bf16[128,24576]{0,1:T(8,128)(2,1)S(1)} %collective-permute-done), kind=kLoop, calls=%fused_computation.2 | loop fusion | flops 25165824 | bytes 25165824 | tf_op jit(solution)/shard_map/concatenate | solution.py:77
  52.0 8.4 %multiply_add_fusion = f32[128,3,8192]{0,2,1:T(8,128)} fusion(bf16[128,6,8192]{0,2,1:T(8,128)(2,1)S(1)} %bitcast.116, f32[8192]{0:T(1024)S(1)} %bitcast.124, f32[8192]{0:T(1024)S(1)} %bitcast.125, f32[8192]{0:T(1024)S(1)} %bitcast.123, f32[8192]{0:T(1024)S(1)} %bitcast.122), kind=kLoop, calls=%fused_computation.5 | loop fusion | flops 34603008 | bytes 37879808 | tf_op jit(solution)/shard_map/add | solution.py:67
  60.4 12.8 %copy.25 = f32[128,3,64,128]{3,2,1,0:T(8,128)} copy(f32[128,3,64,128]{0,3,2,1:T(8,128)} %bitcast.119) | data formatting | bytes 25165824 | tf_op jit(solution)/shard_map/reshape | solution.py:42
  73.2 16.9 %fusion.46 = f32[64,128,3,128]{3,0,2,1:T(8,128)} fusion(f32[128,3,64,128]{3,2,1,0:T(8,128)} %copy.25), kind=kOutput, calls=%fused_computation.99 | convolution fusion | flops 2415976448 | bytes 25165824 | tf_op jit(solution)/shard_map/sfan,ak->sfkn/dot_general | solution.py:45
  90.1 24.0 %add_bitcast_fusion = (f32[128,3,64,128]{3,2,1,0:T(8,128)}, f32[128,3,64,128]{3,2,1,0:T(8,128)}) fusion(f32[64,128,3,128]{3,0,2,1:T(8,128)} %fusion.46, f32[64,128]{1,0:T(8,128)S(1)} %get-tuple-element.15, f32[64,128]{1,0:T(8,128)S(1)} %get-tuple-element.16, f32[128,3,64,128]{3,2,1,0:T(8,128)} %copy.25), kind=kOutput, calls=%fused_computation.4 | convolution fusion | flops 2437996544 | bytes 50397184 | tf_op jit(solution)/shard_map/sfan,ak->sfkn/dot_general | solution.py:44
  114.1 22.5 %fusion = f32[32,128,3,64]{1,0,3,2:T(8,128)S(1)} fusion(f32[128,3,64,128]{3,2,1,0:T(8,128)} %get-tuple-element.8, s32[32]{0:T(128)S(1)} %iota_add_fusion), kind=kOutput, calls=%fused_computation.6 | convolution fusion | flops 1208016896 | bytes 15728768 | tf_op jit(solution)/shard_map/sfkn,nm->mkfs/dot_general | solution.py:58
  136.7 0.0 slice-start.2
  136.7 22.9 %fusion.2 = f32[32,128,3,64]{1,0,3,2:T(8,128)S(1)} fusion(f32[128,3,64,128]{3,2,1,0:T(8,128)} %get-tuple-element.8, s32[32]{0:T(128)S(1)} %iota_add_fusion), kind=kOutput, calls=%fused_computation.8 | convolution fusion | flops 1208016896 | bytes 15728768 | tf_op jit(solution)/shard_map/sfkn,nm->mkfs/dot_general | solution.py:55
  159.5 0.0 slice-done
  159.5 0.0 slice-done.1
  159.6 18.3 %fusion.17 = bf16[32,64,3,128]{3,0,1,2:T(8,128)(2,1)S(1)} fusion(f32[32,128,3,64]{1,0,3,2:T(8,128)S(1)} %fusion.2, f32[128,3,64,128]{3,2,1,0:T(8,128)S(1)} %bitcast.118, s32[32]{0:T(128)S(1)} %iota_add_fusion), kind=kOutput, calls=%fused_computation.52 | convolution fusion | flops 1210376192 | bytes 17301632 | tf_op jit(solution)/shard_map/sfkn,nm->mkfs/dot_general | solution.py:54
  177.9 18.4 %fusion.20 = bf16[32,64,3,128]{3,0,1,2:T(8,128)(2,1)S(1)} fusion(f32[32,128,3,64]{1,0,3,2:T(8,128)S(1)} %fusion, f32[128,3,64,128]{3,2,1,0:T(8,128)S(1)} %bitcast.118, s32[32]{0:T(128)S(1)} %iota_add_fusion), kind=kOutput, calls=%fused_computation.53 | convolution fusion | flops 1210376192 | bytes 17301632 | tf_op jit(solution)/shard_map/sfkn,nm->mkfs/dot_general | solution.py:59
  196.2 0.6 copy.32
  196.8 0.6 copy.29
  198.0 137.2 %all_to_all.5 = bf16[16,128,3,2,128]{4,1,2,3,0:T(8,128)(2,1)S(1)} all-to-all(bf16[16,128,3,2,128]{4,1,2,3,0:T(8,128)(2,1)S(1)} %fusion.39), channel_id=1, replica_groups=mesh['ta'=16,'aa'=2] {'ta'}, dimensions={0} | all-to-all | bytes 6291456 | tf_op jit(solution)/shard_map/all_to_all | solution.py:83
  335.2 0.4 copy.33
  335.6 3.7 copy.36
  339.3 0.0 all-gather.2.cloned.1.call-update
  339.3 1.9 copy-done
  341.2 2.0 fusion.104
  343.2 77.2 %all-gather.2.cloned.1.call-done = bf16[128,48,2,256]{3,1,2,0:T(8,128)(2,1)} async-done(((bf16[128,48,2,128]{3,1,2,0:T(8,128)(2,1)}), bf16[128,48,2,256]{3,1,2,0:T(8,128)(2,1)}) %all-gather.2.cloned.1.call-update) | async-done | bytes 6291472 | tf_op jit(solution)/shard_map/all_gather | solution.py:89
  420.4 16.4 %bitcast_multiply_fusion = f32[128,256,256]{1,2,0:T(8,128)} fusion(bf16[128,48,2,256]{3,1,2,0:T(8,128)(2,1)} %all-gather.2.cloned.1.call-done, bf16[128,48,1,128]{3,1,2,0:T(8,128)(2,1)} %get-tuple-element.10, bf16[128,48,1,128]{3,1,2,0:T(8,128)(2,1)} %get-tuple-element.9, bf16[128,48,2,128]{3,1,2,0:T(8,128)(2,1)S(1)} %copy-done), kind=kOutput, calls=%fused_computation.1 | convolution fusion | flops 1637875712 | bytes 46137344 | tf_op jit(solution)/shard_map/cfpi,cfpj->cij/dot_general | solution.py:33
  436.8 17.7 %fusion.103 = (f32[128,128,256]{1,2,0:T(8,128)S(1)}, f32[128,128,256]{1,2,0:T(8,128)}) fusion(f32[128,256,256]{1,2,0:T(8,128)} %bitcast_multiply_fusion), kind=kLoop, calls=%fused_computation.154 | loop fusion | bytes 67108864 | tf_op jit(solution)/shard_map/slice | solution.py:90
  454.6 18.3 %pad_maximum_fusion = f32[128,128,512]{1,2,0:T(8,128)} fusion(f32[128,128,256]{1,2,0:T(8,128)} %get-tuple-element.6, f32[128,128,256]{1,2,0:T(8,128)S(1)} %get-tuple-element.5), kind=kLoop, calls=%fused_computation | loop fusion | flops 8388608 | bytes 67108864 | tf_op jit(solution)/shard_map/concatenate | solution.py:90
  472.9 33.4 %copy.38 = f32[128,128,512]{2,1,0:T(8,128)} copy(f32[128,128,512]{1,2,0:T(8,128)} %pad_maximum_fusion) | data formatting | bytes 67108864 | tf_op jit(solution)/shard_map/concatenate | solution.py:90
  (23 shorter events, 0.4 us)
Async XLA Ops:
  6.5 11.6 %copy-start.1 = (f32[4,8192]{1,0:T(4,128)S(1)}, f32[4,8192]{1,0:T(4,128)}, u32[]{:S(2)}) copy-start(f32[4,8192]{1,0:T(4,128)} %param.3) | copy-start | bytes 393220
  6.5 413.9 %all-gather.2.cloned.1.call-start = ((), (), s32[]{:S(2)}) async-start(), calls=%async_computation.1 | async-start | bytes 9437184 | tf_op jit(solution)/shard_map/all_gather | solution.py:89
  15.2 12.4 %collective-permute-start = (bf16[128,24576]{0,1:T(8,128)(2,1)}, bf16[128,24576]{0,1:T(8,128)(2,1)S(1)}, u32[]{:S(2)}, u32[]{:S(2)}) collective-permute-start(bf16[128,24576]{0,1:T(8,128)(2,1)} %copy.23), channel_id=1, source_target_pairs={{0,2},{2,4},{4,6},{6,8},{8,10},{10,12},{12,14},{14,16},{16,18},{18... | collective-permute-start | bytes 18874376 | tf_op jit(solution)/shard_map/ppermute | solution.py:16
  114.1 45.4 %slice-start = ((s8[12582912]{0:T(1024)(128)(4,1)}), s8[4194304]{0:T(1024)(128)(4,1)S(1)}, s32[]{:S(2)}) async-start(s8[12582912]{0:T(1024)(128)(4,1)} %bitcast.117), calls=%async_computation.2 | async-start | bytes 8388608
  114.1 45.4 %slice-start.1 = ((s8[12582912]{0:T(1024)(128)(4,1)}), s8[4194304]{0:T(1024)(128)(4,1)S(1)}, s32[]{:S(2)}) async-start(s8[12582912]{0:T(1024)(128)(4,1)} %bitcast.117), calls=%async_computation.3 | async-start | bytes 8388608
  136.7 22.9 %slice-start.2 = ((s8[12582912]{0:T(1024)(128)(4,1)}), s8[4194304]{0:T(1024)(128)(4,1)S(1)}, s32[]{:S(2)}) async-start(s8[12582912]{0:T(1024)(128)(4,1)} %bitcast.117), calls=%async_computation.4 | async-start | bytes 8388608
  339.3 1.9 copy-start
Sparse Core Ops, SparseCore 0:
  339.5 80.8 all-gather.1
